TPU v7x, 32 devices: a whole 2x2x4 slice. The times are simulated.
32 devices in a mesh: dp: 8 (over y, x, core), expert: 4 (over z).
Axes of the slice: x: 2, y: 2, z: 4, core: 2. Of those that a mesh axis runs over, the one named last changes fastest.
Arguments:
- tokens: bfloat16 [4096, 1792], P(('dp', 'expert')), may hold values from -6 to 6
- routes: int32 [4096, 2], P(('dp', 'expert')), may hold values from 0 to 3, all different within a row; in each aligned block of 128 rows (0 to 127, 128 to 255, ...) at most 128 rows name the same one
- gates: float32 [4096, 2], P(('dp', 'expert')), may hold values from 0.25 to 1
- grad_hidden: bfloat16 [4096, 2, 512], P(('dp', 'expert')), may hold values from -4 to 4
- w_in: bfloat16 [4, 1792, 512], P('expert', 'dp'), may hold values from -0.25 to 0.25
- error: bfloat16 [8, 4, 1792, 512], P('dp', 'expert'), may hold values from -6 to 6
- q_seed: float32 [4, 512, 32], P('expert'), may hold values from -6 to 6
Outputs:
- grad_tokens: bfloat16 [4096, 1792], P(('dp', 'expert'))
- error_next: bfloat16 [8, 4, 1792, 512], P('dp', 'expert')
- weight_grad: float32 [4, 1792, 512], P('expert', 'dp')
Inputs may be any that keep to these rules, and one draw needn't show every extreme that they name: `routes`: in the rows of one device no expert is named by more than 128 rows, a bound that some block reaches; the two experts of a row differ.
All inputs are finite; a program needn't handle non-finite values.
Results may differ from a plain program's by a relative error of at most 0.014.
Values may be sent and summed in bfloat16 or wider, within the bound.
A program may use at most 64 MiB of HBM per device.

v0:
```python
import jax
import jax.numpy as jnp
from jax import lax
from jax.sharding import PartitionSpec as P

highest = lax.Precision.HIGHEST


def slopes(pre_act):
    squashed = jax.nn.sigmoid(pre_act)
    return squashed * (1.0 + pre_act * (1.0 - squashed))


def body(tokens, routes, gates, grad_hidden, w_in, error, q_seed):
    experts = lax.axis_size("expert")
    replicas = lax.axis_size("dp")
    row_count = tokens.shape[0]
    width = tokens.shape[1]
    hidden = grad_hidden.shape[2]
    capacity = 4 * row_count // experts
    chosen = routes.reshape(-1)
    matches = (chosen[:, None] == jnp.arange(experts, dtype=jnp.int32)[None, :]).astype(jnp.int32)
    earlier = jnp.cumsum(matches, axis=0) - matches
    position = chosen * capacity + jnp.sum(earlier * matches, axis=1)
    placer = (jnp.arange(experts * capacity, dtype=jnp.int32)[:, None] == position[None, :]).astype(
        jnp.bfloat16
    )
    gate_flat = gates.reshape(-1)
    scaled = (jnp.repeat(tokens, 2, axis=0).astype(jnp.float32) * gate_flat[:, None]).astype(
        jnp.bfloat16
    )
    sent_rows = jnp.dot(placer, scaled, preferred_element_type=jnp.float32).astype(jnp.bfloat16)
    sent_grad = jnp.dot(
        placer, grad_hidden.reshape(2 * row_count, hidden), preferred_element_type=jnp.float32
    ).astype(jnp.bfloat16)
    sent_rows = sent_rows.reshape(experts, capacity, width)
    sent_grad = sent_grad.reshape(experts, capacity, hidden)
    weight_part = w_in[0]
    arrived, arrived_grad = (
        lax.all_to_all(sent_rows, "expert", split_axis=0, concat_axis=0, tiled=True),
        lax.all_to_all(sent_grad, "expert", split_axis=0, concat_axis=0, tiled=True),
    )
    arrived = arrived.reshape(experts * capacity, width)
    arrived_grad = arrived_grad.reshape(experts * capacity, hidden)
    pre_act = jnp.dot(
        arrived,
        lax.all_gather(weight_part, "dp", axis=0, tiled=True),
        preferred_element_type=jnp.float32,
    )
    grad_pre = (arrived_grad.astype(jnp.float32) * slopes(pre_act)).astype(jnp.bfloat16)
    weight_term = lax.dot_general(
        arrived, grad_pre, (((0,), (0,)), ((), ())), preferred_element_type=jnp.float32
    )
    grad_rows = lax.dot_general(
        grad_pre,
        lax.all_gather(weight_part, "dp", axis=0, tiled=True),
        (((1,), (1,)), ((), ())),
        preferred_element_type=jnp.float32,
    )
    sending = grad_rows.astype(jnp.bfloat16).reshape(experts, capacity, width)
    returned = lax.all_to_all(sending, "expert", split_axis=0, concat_axis=0, tiled=True).reshape(
        experts * capacity, width
    )
    picked = jnp.take(returned, position, axis=0).astype(jnp.float32) * gate_flat[:, None]
    grad_tokens = jnp.sum(picked.reshape(row_count, 2, width), axis=1).astype(jnp.bfloat16)
    merged = weight_term + error[0, 0].astype(jnp.float32)
    q_start = q_seed[0]
    local_factor = lax.dot_general(q_start, merged, (((0,), (1,)), ((), ())), precision=highest)
    part_rows = lax.psum_scatter(local_factor, "dp", scatter_dimension=1, tiled=True) / replicas
    gram_matrix = lax.psum(jnp.dot(part_rows, part_rows.T, precision=highest), "dp")
    lower_factor = jnp.linalg.cholesky(gram_matrix)
    part_basis = jax.scipy.linalg.solve_triangular(lower_factor, part_rows, lower=True)
    basis = lax.all_gather(part_basis, "dp", axis=1, tiled=True)
    q_factor = (
        lax.psum(jnp.dot(basis, merged, precision=highest).astype(jnp.bfloat16), "dp").astype(
            jnp.float32
        )
        / replicas
    )
    low_rank = lax.dot_general(basis, q_factor, (((0,), (0,)), ((), ())), precision=highest)
    error_next = (merged - low_rank).astype(jnp.bfloat16)[None, None]
    shard_rows = width // replicas
    weight_grad = lax.dynamic_slice_in_dim(
        low_rank, lax.axis_index("dp") * shard_rows, shard_rows, 0
    )[None]
    return (grad_tokens, error_next, weight_grad)


def solution(mesh):
    placed = (
        P(("dp", "expert"), None),
        P(("dp", "expert"), None),
        P(("dp", "expert"), None),
        P(("dp", "expert"), None, None),
        P("expert", "dp", None),
        P("dp", "expert", None, None),
        P("expert", None, None),
    )
    return jax.shard_map(
        body,
        mesh=mesh,
        in_specs=placed,
        out_specs=(
            P(("dp", "expert"), None),
            P("dp", "expert", None, None),
            P("expert", "dp", None),
        ),
        check_vma=False,
    )
```

profile of v0, /device:TPU:0, one launch (start us, length us, event | category | flops | bytes accessed | tf_op | source)
XLA Modules:
  0.0 212.2 jit_solution(1840900786812910726)
XLA Ops:
  7.2 0.8 copy.36
  8.0 0.1 eq.39
  8.2 0.1 reshape.117
  8.3 1.1 reshape.119
  9.4 1.2 reduce-window.6
  10.7 0.1 copy.38
  11.0 1.1 convolution_convert_fusion.2
  12.1 6.3 %all-to-all-start = ((bf16[4,128,512]{2,1,0:T(8,128)(2,1)}), bf16[4,128,512]{2,1,0:T(8,128)(2,1)S(1)}, u32[]{:S(2)}, u32[]{:S(2)}) async-start(bf16[4,128,512]{2,1,0:T(8,128)(2,1)} %bitcast.2), calls=%async_computation | async-start | bytes 1048576 | tf_op jit(solution)/shard_map/all_to_all | solution.py:41
  18.5 0.7 all-gather.4.cloned.1.call-update
  19.2 1.7 broadcast_in_dim.25
  20.9 2.6 %convert_element_type.64 = f32[256,1792]{1,0:T(8,128)S(1)} reshape(f32[128,2,1792]{2,1,0:T(2,128)} %broadcast_in_dim.25) | data formatting | bytes 3670016 | tf_op jit(solution)/shard_map/convert_element_type | solution.py:29
  23.5 0.1 copy.42
  23.6 0.1 mul.66
  23.8 2.0 convolution_convert_fusion
  25.7 7.3 %all-to-all-done = bf16[4,128,512]{2,1,0:T(8,128)(2,1)S(1)} async-done(((bf16[4,128,512]{2,1,0:T(8,128)(2,1)}), bf16[4,128,512]{2,1,0:T(8,128)(2,1)S(1)}, u32[]{:S(2)}, u32[]{:S(2)}) %all-to-all-start) | async-done | bytes 524320 | tf_op jit(solution)/shard_map/all_to_all | solution.py:41
  33.0 3.7 %all-to-all-start.1 = ((bf16[4,128,1792]{2,1,0:T(8,128)(2,1)}), bf16[4,128,1792]{2,1,0:T(8,128)(2,1)S(1)}, u32[]{:S(2)}, u32[]{:S(2)}) async-start(bf16[4,128,1792]{2,1,0:T(8,128)(2,1)} %bitcast.74), calls=%async_computation.1 | async-start | bytes 3670016 | tf_op jit(solution)/shard_map/all_to_all | solution.py:40
  36.8 0.1 reduce_sum.23
  36.9 0.1 copy.43
  37.0 0.1 mul.72
  37.2 41.6 %all-to-all-done.1 = bf16[4,128,1792]{2,1,0:T(8,128)(2,1)S(1)} async-done(((bf16[4,128,1792]{2,1,0:T(8,128)(2,1)}), bf16[4,128,1792]{2,1,0:T(8,128)(2,1)S(1)}, u32[]{:S(2)}, u32[]{:S(2)}) %all-to-all-start.1) | async-done | bytes 1835040 | tf_op jit(solution)/shard_map/all_to_all | solution.py:40
  78.8 3.0 %fusion.4 = bf16[512,512]{1,0:T(8,128)(2,1)S(1)} fusion(bf16[512,512]{1,0:T(8,128)(2,1)S(1)} %bitcast.77, bf16[512,1792]{1,0:T(8,128)(2,1)S(1)} %bitcast.72, bf16[1,1792,512]{2,1,0:T(8,128)(2,1)} %all-gather.4.cloned.1.call-done), kind=kOutput, calls=%fused_computation.17 | convolution fusion | flops 942145536 | bytes 4718592 | tf_op jit(solution)/shard_map/dot_general | solution.py:45
  81.8 1.2 convert_add_fusion
  83.0 1.8 copy-done.1
  84.8 3.4 %convolution_bitcast_fusion = f32[32,1792]{1,0:T(8,128)S(1)} fusion(f32[1792,512]{1,0:T(8,128)S(1)} %convert_add_fusion, f32[1,512,32]{1,2,0:T(8,128)S(1)} %copy-done), kind=kOutput, calls=%fused_computation.5 | convolution fusion | flops 352321536 | bytes 3964928 | tf_op jit(solution)/shard_map/dot_general | solution.py:68
  88.2 1.2 copy.49
  89.5 3.9 %convolution_convert_fusion.1 = bf16[512,1792]{1,0:T(8,128)(2,1)} fusion(bf16[512,512]{1,0:T(8,128)(2,1)S(1)} %fusion.4, bf16[1,1792,512]{2,1,0:T(8,128)(2,1)} %all-gather.4.cloned.1.call-done), kind=kOutput, calls=%fused_computation.4 | convolution fusion | flops 940441600 | bytes 4194304 | tf_op jit(solution)/shard_map/dot_general | solution.py:54
  93.4 3.6 %all-to-all-start.2 = ((bf16[4,128,1792]{2,1,0:T(8,128)(2,1)}), bf16[4,128,1792]{2,1,0:T(8,128)(2,1)S(1)}, u32[]{:S(2)}, u32[]{:S(2)}) async-start(bf16[4,128,1792]{2,1,0:T(8,128)(2,1)} %bitcast.76), calls=%async_computation.2 | async-start | bytes 3670016 | tf_op jit(solution)/shard_map/all_to_all | solution.py:61
  97.1 0.1 copy.41
  97.2 27.0 %reduce-scatter.4.cloned.1.call-done = f32[224,32]{1,0:T(8,128)} async-done(((f32[1792,32]{1,0:T(8,128)}), f32[224,32]{1,0:T(8,128)}) %reduce-scatter.4.cloned.1.call-update) | async-done | bytes 28688
  124.2 1.0 copy.50
  125.1 0.2 fusion.16
  125.3 23.2 %psum.14 = f32[32,32]{0,1:T(8,128)S(1)} all-reduce(f32[32,32]{0,1:T(8,128)S(1)} %fusion.16), channel_id=1, replica_groups=mesh['dp'=8,'expert'=4] {'dp'}, use_global_device_ids=true, to_apply=%region_5.6 | all-reduce | flops 1024 | bytes 8192 | tf_op jit(solution)/shard_map/psum | solution.py:70
  148.6 2.9 %cholesky.16 = f32[32,32]{1,0:T(8,128)S(1)} custom-call(f32[32,32]{1,0:T(8,128)S(1)} %fusion.20), custom_call_target="Cholesky" | custom-call | tf_op jit(solution)/shard_map/jit(cholesky)/cholesky | solution.py:71
  151.6 0.6 compare_reduce_fusion
  152.2 0.7 fusion.18
  152.9 2.4 %custom-call.7 = f32[1,32,32]{1,2,0:T(8,128)S(1)} custom-call(f32[1,32,32]{2,1,0:T(8,128)S(1)} %fusion.18), custom_call_target="InvertDiagBlocksLowerTriangular" | custom-call | tf_op jit(solution)/shard_map/jit(_solve_triangular)/triangular_solve | solution.py:72
  155.3 0.2 convolution_bitcast_fusion.1
  155.6 9.6 %all-gather.1 = f32[8,224,32]{1,2,0:T(8,128)S(1)} all-gather(f32[1,224,32]{1,2,0:T(8,128)S(1)} %convolution_bitcast_fusion.1), channel_id=1, replica_groups=mesh['dp'=8,'expert'=4] {'dp'}, dimensions={0}, use_global_device_ids=true | all-gather | bytes 258048 | tf_op jit(solution)/shard_map/all_gather | solution.py:73
  165.2 0.2 copy.47
  165.3 0.1 reshape.137
  165.5 4.2 %convolution_convert_fusion.3 = bf16[32,512]{1,0:T(8,128)(2,1)S(1)} fusion(f32[1792,32]{0,1:T(8,128)S(1)} %reshape.137, f32[1792,512]{1,0:T(8,128)} %copy-done.1), kind=kOutput, calls=%fused_computation.14 | convolution fusion | flops 352337920 | bytes 3932160 | tf_op jit(solution)/shard_map/dot_general | solution.py:75
  169.7 23.6 %psum.15 = bf16[32,512]{1,0:T(8,128)(2,1)S(1)} all-reduce(bf16[32,512]{1,0:T(8,128)(2,1)S(1)} %convolution_convert_fusion.3), channel_id=1, replica_groups=mesh['dp'=8,'expert'=4] {'dp'}, use_global_device_ids=true, to_apply=%region_8.9 | all-reduce | flops 16384 | bytes 65536 | tf_op jit(solution)/shard_map/psum | solution.py:75
  193.3 3.1 %fusion.11 = f32[1792,512]{1,0:T(8,128)S(1)} fusion(f32[1792,32]{0,1:T(8,128)S(1)} %reshape.137, bf16[32,512]{1,0:T(8,128)(2,1)S(1)} %psum.15), kind=kOutput, calls=%fused_computation.24 | convolution fusion | flops 352354304 | bytes 3932160 | tf_op jit(solution)/shard_map/dot_general | solution.py:80
  196.4 0.8 dynamic-slice_bitcast_fusion
  197.2 2.0 fusion
  199.2 1.3 gather_fusion
  200.5 0.3 gather.7
  200.9 4.5 %multiply_reduce_fusion = bf16[128,1792]{1,0:T(8,128)(2,1)} fusion(bf16[128,2,1792]{2,1,0:T(2,128)(2,1)S(1)} %gather.7, pred[128,2]{1,0:T(8,128)(4,1)S(1)} %copy.41, f32[128,2]{1,0:T(8,128)S(1)} %copy.42), kind=kLoop, calls=%fused_computation.10 | loop fusion | flops 1605632 | bytes 1377536 | tf_op jit(solution)/shard_map/reduce_sum | solution.py:65
  (34 shorter events, 0.6 us)
Async XLA Ops:
  7.2 77.6 %copy-start = (f32[1,512,32]{1,2,0:T(8,128)S(1)}, f32[1,512,32]{1,2,0:T(8,128)}, u32[]{:S(2)}) copy-start(f32[1,512,32]{1,2,0:T(8,128)} %param.13) | copy-start | bytes 196612
  7.2 12.0 %copy-start.4 = (bf16[128,1792]{1,0:T(8,128)(2,1)S(1)}, bf16[128,1792]{1,0:T(8,128)(2,1)}, u32[]{:S(2)}) copy-start(bf16[128,1792]{1,0:T(8,128)(2,1)} %param.7) | copy-start | bytes 1376260
  12.1 20.8 %all-to-all-start = ((bf16[4,128,512]{2,1,0:T(8,128)(2,1)}), bf16[4,128,512]{2,1,0:T(8,128)(2,1)S(1)}, u32[]{:S(2)}, u32[]{:S(2)}) async-start(bf16[4,128,512]{2,1,0:T(8,128)(2,1)} %bitcast.2), calls=%async_computation | async-start | bytes 1048576 | tf_op jit(solution)/shard_map/all_to_all | solution.py:41
  18.5 60.3 %all-gather.4.cloned.1.call-start = ((), (), s32[]{:S(2)}) async-start(), calls=%async_computation.4 | async-start | bytes 2064384 | tf_op jit(solution)/shard_map/all_gather | solution.py:47
  20.9 2.6 %copy-start.6 = (f32[128,2]{0,1:T(2,128)S(1)}, f32[128,2]{0,1:T(2,128)}, u32[]{:S(2)}) copy-start(f32[128,2]{0,1:T(2,128)} %param.9) | copy-start | bytes 3076
  33.0 3.9 %copy-start.5 = (s32[128,2]{0,1:T(2,128)S(1)}, s32[128,2]{0,1:T(2,128)}, u32[]{:S(2)}) copy-start(s32[128,2]{0,1:T(2,128)} %param.8) | copy-start | bytes 3076
  33.0 45.8 %all-to-all-start.1 = ((bf16[4,128,1792]{2,1,0:T(8,128)(2,1)}), bf16[4,128,1792]{2,1,0:T(8,128)(2,1)S(1)}, u32[]{:S(2)}, u32[]{:S(2)}) async-start(bf16[4,128,1792]{2,1,0:T(8,128)(2,1)} %bitcast.74), calls=%async_computation.1 | async-start | bytes 3670016 | tf_op jit(solution)/shard_map/all_to_all | solution.py:40
  36.7 87.5 %reduce-scatter.4.cloned.1.call-start = ((), (), s32[]{:S(2)}) async-start(), calls=%async_computation.5 | async-start | bytes 1032192
  78.8 3.0 %copy-start.3 = (bf16[1,1,1792,512]{3,2,1,0:T(8,128)(2,1)S(1)}, bf16[1,1,1792,512]{3,2,1,0:T(8,128)(2,1)}, u32[]{:S(2)}) copy-start(bf16[1,1,1792,512]{3,2,1,0:T(8,128)(2,1)} %param.12) | copy-start | bytes 5505028
  83.0 1.8 copy-start.1
  93.4 105.8 %all-to-all-start.2 = ((bf16[4,128,1792]{2,1,0:T(8,128)(2,1)}), bf16[4,128,1792]{2,1,0:T(8,128)(2,1)S(1)}, u32[]{:S(2)}, u32[]{:S(2)}) async-start(bf16[4,128,1792]{2,1,0:T(8,128)(2,1)} %bitcast.76), calls=%async_computation.2 | async-start | bytes 3670016 | tf_op jit(solution)/shard_map/all_to_all | solution.py:61
  193.3 3.9 %copy-start.2 = (f32[1792,512]{1,0:T(8,128)S(1)}, f32[1792,512]{1,0:T(8,128)}, u32[]{:S(2)}) copy-start(f32[1792,512]{1,0:T(8,128)} %copy-done.1) | copy-start | bytes 11010052
Sparse Core Ops, SparseCore 0:
  21.2 28.1 all-gather.3
  89.6 34.5 reduce-scatter.3
where the time goes:
time: 213 us; the launch traced here: 212 us
  waiting for transfers between devices  76.5 us (36%)
  blocking collectives  56.4 us (26%)
  matrix products  22.3 us (10%)
  other arithmetic  14.6 us (7%)
  local copies, waits for them, and re-layouts  14.4 us (7%)
  between operations  14.3 us (7%)
  starting transfers between devices  13.7 us (6%)
    all_to_all x1, waiting for transfers between devices, body(): lax.all_to_all(sent_rows, 'expert', split_axis=0, concat_axis=0, tiled=True)  41.6 us
    unnamed x3, waiting for transfers between devices  27.7 us
    psum x1, blocking collectives, body(): lax.psum(jnp.dot(basis, merged, precision=highest).astype(jnp.bfloat16),...  23.6 us
    psum x1, blocking collectives, body(): lax.psum(jnp.dot(part_rows, part_rows.T, precision=highest), 'dp')  23.2 us
    all_gather x1, blocking collectives, body(): basis = lax.all_gather(part_basis, 'dp', axis=1, tiled=True)  9.58 us
    all_to_all x1, waiting for transfers between devices, body(): lax.all_to_all(sent_grad, 'expert', split_axis=0, concat_axis=0, tiled=True)  7.26 us
    all_to_all x1, starting transfers between devices, body(): lax.all_to_all(sent_grad, 'expert', split_axis=0, concat_axis=0, tiled=True)  6.34 us
    unnamed x19, local copies, waits for them, and re-layouts  5.1 us
  transfers between devices with their start and end apart: 5, of which 3 were waited for; matrix products, arithmetic and copies ran while one was open for 14% of the time, Pallas kernels for 0%

commit v1 on v0

v1 whole, which is shorter than its diff:
```python
import functools

import jax
import jax.numpy as jnp
from jax import lax
from jax.experimental import pallas as pl
from jax.experimental.pallas import tpu as pltpu
from jax.sharding import PartitionSpec as P

HI = lax.Precision.HIGHEST
MESH = pl.DeviceIdType.MESH
F32 = jnp.float32
BF16 = jnp.bfloat16


def slopes(pre_act):
    squashed = 1.0 / (1.0 + jnp.exp(-pre_act))
    return squashed * (1.0 + pre_act * (1.0 - squashed))


def inverse_factor(gram):
    rank = gram.shape[0]
    rows = lax.broadcasted_iota(jnp.int32, (rank, rank), 0)
    cols = lax.broadcasted_iota(jnp.int32, (rank, rank), 1)
    left = gram
    right = (rows == cols).astype(F32)
    row_id = lax.broadcasted_iota(jnp.int32, (rank, 1), 0)
    for i in range(rank):
        inv = 1.0 / jnp.sqrt(left[i : i + 1, i : i + 1])
        row_l = left[i : i + 1, :] * inv
        row_r = right[i : i + 1, :] * inv
        col = jnp.where(row_id > i, left[:, i : i + 1] * inv, 0.0)
        here = row_id == i
        left = jnp.where(here, row_l, left - col * row_l)
        right = jnp.where(here, row_r, right - col * row_r)
    return right


def kernel(dims, tok_ref, gh_ref, gate_ref, w_ref, err_hbm, qt_ref,
           gt_out, err_out, wg_out,
           tok_all, gh_all, gate_all, w_all, x_all, gp_all, err_v, merged, back, ret,
           fbuf, rsbuf, agbuf, tbuf,
           err_sem, tok_s, tok_r, gh_s, gh_r, gate_s, gate_r, w_s, w_r,
           f_s, f_r, a_s, a_r, t_s, t_r, b_s, b_r):
    E, N, rp, chunk, gather_w = dims
    z = lax.axis_index("expert")
    me = lax.axis_index("dp")
    tokens, width = tok_ref.shape
    shard = width // N
    rank = qt_ref.shape[0]
    groups = width // 128

    def other(axis, size, k):
        return lax.rem(lax.axis_index(axis) + k, size)

    def loop(size, fn, start=1):
        def step(k, c):
            fn(k)
            return c
        lax.fori_loop(start, size, step, 0)

    err_copy = pltpu.make_async_copy(err_hbm.at[0, 0], err_v, err_sem)
    err_copy.start()

    barrier = pltpu.get_barrier_semaphore()
    loop(E, lambda k: pl.semaphore_signal(
        barrier, inc=1, device_id={"expert": other("expert", E, k)}, device_id_type=MESH))
    loop(N, lambda k: pl.semaphore_signal(
        barrier, inc=1, device_id={"dp": other("dp", N, k)}, device_id_type=MESH))
    pl.semaphore_wait(barrier, E - 1 + N - 1)

    def rdma(src, dst, s, r, axis, peer):
        return pltpu.make_async_remote_copy(
            src_ref=src, dst_ref=dst, send_sem=s, recv_sem=r,
            device_id={axis: peer}, device_id_type=MESH)

    def gate_copy(p, slot, k):
        return rdma(gate_ref.at[p], gate_all.at[slot], gate_s.at[k], gate_r.at[slot], "expert", p)

    def gh_copy(p, slot, k):
        return rdma(gh_ref.at[p], gh_all.at[slot], gh_s.at[k], gh_r.at[slot], "expert", p)

    def tok_copy(j, nb, slot):
        src = tok_all.at[j]
        return rdma(src, tok_all.at[j], tok_s.at[slot], tok_r.at[j], "expert", nb)

    def w_copy(p, slot, k):
        return rdma(w_ref, w_all.at[pl.ds(pl.multiple_of(slot * shard, 16), shard)],
                    w_s.at[k], w_r.at[slot], "dp", p)

    def each(p_axis, size, copy, act):
        mine = lax.axis_index(p_axis)

        def fn(k):
            p = other(p_axis, size, k)
            if act == "start":
                copy(p, mine, k).start()
            elif act == "recv":
                copy(p, p, k).wait_recv()
            else:
                copy(p, mine, k).wait_send()
        loop(size, fn)

    def forward(s, mode):
        for d, dirn in enumerate((1, -1)):
            j = z - dirn * s
            nb = z + dirn
            inside = (j >= 0) & (j < E)
            linked = inside & (nb >= 0) & (nb < E)
            slot = d * E + s
            if mode == "first":
                @pl.when(linked)
                def _():
                    rdma(tok_ref, tok_all.at[z], tok_s.at[slot], tok_r.at[z], "expert", nb).start()
            elif mode == "relay":
                @pl.when(inside)
                def _():
                    tok_copy(j, nb, slot).wait_recv()

                @pl.when(linked)
                def _():
                    tok_copy(j, nb, slot).start()
            else:
                @pl.when(linked)
                def _():
                    tok_copy(j, nb, slot).wait_send()

    each("expert", E, gate_copy, "start")
    forward(0, "first")
    each("expert", E, gh_copy, "start")
    if gather_w:
        each("dp", N, w_copy, "start")
        w_all[pl.ds(pl.multiple_of(me * shard, 16), shard), :] = w_ref[...]
        weights = w_all
    else:
        weights = w_ref
    tok_all[z] = tok_ref[...]
    gh_all[z] = gh_ref[z]
    gate_all[z] = gate_ref[z]
    each("expert", E, gate_copy, "recv")
    forward(1, "relay")
    if gather_w:
        each("dp", N, w_copy, "recv")

    def back_copy(p, slot, k):
        return rdma(back.at[p], ret.at[slot], b_s.at[p], b_r.at[slot], "expert", p)

    def block(i, c):
        s = i // 2
        d = lax.rem(i, 2)

        @pl.when((d == 0) & (s >= 2))
        def _():
            forward(s, "relay")

        j = z - (1 - 2 * d) * s

        @pl.when((j >= 0) & (j < E) & (i != 1))
        def _():
            @pl.when(s > 0)
            def _():
                gh_copy(j, j, 0).wait_recv()
            g = jnp.transpose(gate_all[j])[:, :1]
            x = (tok_all[j].astype(F32) * g).astype(BF16)
            x_all[j] = x
            pre = jnp.dot(x, weights[...], preferred_element_type=F32)
            gp = (gh_all[j].astype(F32) * slopes(pre)).astype(BF16)
            gp_all[j] = gp
            rows = lax.dot_general(gp, weights[...], (((1,), (1,)), ((), ())),
                                   preferred_element_type=F32)
            back[j] = (rows * g).astype(BF16)

            @pl.when(s > 0)
            def _():
                back_copy(j, z, 0).start()
        return c
    lax.fori_loop(0, 2 * E, block, 0)

    err_copy.wait()
    if fbuf.shape[0] > groups * rank:
        fbuf[...] = jnp.zeros_like(fbuf)

    def merge(c):
        cols = pl.ds(pl.multiple_of(c * chunk, chunk), chunk)
        x = x_all[:, :, cols].reshape(E * tokens, chunk)
        gp = gp_all[...].reshape(E * tokens, gp_all.shape[2])
        m = lax.dot_general(x, gp, (((0,), (0,)), ((), ())), preferred_element_type=F32)
        m = m + err_v[cols, :].astype(F32)
        merged[cols, :] = m
        f = lax.dot_general(qt_ref[...], m, (((1,), (1,)), ((), ())), precision=HI,
                            preferred_element_type=F32)
        for h in range(chunk // 128):
            fbuf[pl.ds(pl.multiple_of((c * (chunk // 128) + h) * rank, rank), rank), :] = (
                f[:, h * 128 : (h + 1) * 128])
    loop(width // chunk, merge, 0)

    def f_copy(p, slot, k):
        return rdma(fbuf.at[pl.ds(pl.multiple_of(p * rp, 8), rp)], rsbuf.at[slot],
                    f_s.at[k], f_r.at[slot], "dp", p)

    def a_copy(p, slot, k):
        part = agbuf.at[pl.ds(pl.multiple_of(slot * rp, 8), rp)]
        return rdma(part, part, a_s.at[k], a_r.at[slot], "dp", p)

    def t_copy(p, slot, k):
        return rdma(tbuf.at[slot], tbuf.at[slot], t_s.at[k], t_r.at[slot], "dp", p)

    own = pl.ds(pl.multiple_of(me * rp, 8), rp)
    each("dp", N, f_copy, "start")
    rsbuf[me] = fbuf[own, :]
    each("dp", N, f_copy, "recv")
    agbuf[own, :] = jnp.sum(rsbuf[...], axis=0) * (1.0 / N)
    each("dp", N, a_copy, "start")
    each("dp", N, a_copy, "recv")
    factor = jnp.concatenate([agbuf[c * rank : (c + 1) * rank, :] for c in range(groups)], axis=1)
    gram = lax.dot_general(factor, factor, (((1,), (1,)), ((), ())), precision=HI,
                           preferred_element_type=F32)
    basis = jnp.dot(inverse_factor(gram), factor, precision=HI, preferred_element_type=F32)
    right = jnp.dot(basis, merged[...], precision=HI, preferred_element_type=F32)
    tbuf[me] = right.astype(BF16)
    each("dp", N, t_copy, "start")
    basis_t = jnp.transpose(basis)
    each("dp", N, t_copy, "recv")
    q_factor = jnp.sum(tbuf[...].astype(F32), axis=0) * (1.0 / N)

    for c in range(width // chunk):
        cols = pl.ds(c * chunk, chunk)
        low = jnp.dot(basis_t[c * chunk : (c + 1) * chunk, :], q_factor, precision=HI,
                      preferred_element_type=F32)
        err_out[0, 0, cols, :] = (merged[cols, :] - low).astype(BF16)
        merged[cols, :] = low
    wg_out[0] = merged[pl.ds(pl.multiple_of(me * shard, 8), shard), :]

    each("expert", E, back_copy, "recv")
    ret[z] = back[z]
    total = ret[0].astype(F32)
    for j in range(1, E):
        total = total + ret[j].astype(F32)
    gt_out[...] = total.astype(BF16)

    forward_first = [(0, 1), (1, -1)]
    for d, dirn in forward_first:
        nb = z + dirn

        @pl.when((nb >= 0) & (nb < E))
        def _():
            rdma(tok_ref, tok_all.at[z], tok_s.at[d * E], tok_r.at[z], "expert", nb).wait_send()
    loop(E, lambda s: forward(s, "drain"))
    each("expert", E, gate_copy, "send")
    each("expert", E, gh_copy, "send")
    if gather_w:
        each("dp", N, w_copy, "send")
    each("expert", E, back_copy, "send")
    each("dp", N, f_copy, "send")
    each("dp", N, a_copy, "send")
    each("dp", N, t_copy, "send")


def body(tokens, routes, gates, grad_hidden, w_in, error, q_seed):
    E = lax.axis_size("expert")
    N = lax.axis_size("dp")
    rows, width = tokens.shape
    hidden = grad_hidden.shape[2]
    rank = q_seed.shape[2]
    shard = width // N
    ids = jnp.arange(E, dtype=jnp.int32)
    hit0 = routes[None, :, 0] == ids[:, None]
    hit1 = routes[None, :, 1] == ids[:, None]
    gate_sel = jnp.where(hit0, gates[None, :, 0], jnp.where(hit1, gates[None, :, 1], 0.0))
    gate_sel = jnp.broadcast_to(gate_sel[:, None, :], (E, 8, rows))
    zero = jnp.zeros((), BF16)
    gh_sel = jnp.where(hit0[:, :, None], grad_hidden[None, :, 0, :],
                       jnp.where(hit1[:, :, None], grad_hidden[None, :, 1, :], zero))
    gather_w = shard % 16 == 0
    weight = w_in[0] if gather_w else lax.all_gather(w_in[0], "dp", axis=0, tiled=True)
    chunk = 256 if width % 256 == 0 else 128
    total_rows = width // 128 * rank
    rp = -(-total_rows // N)
    rp = -(-rp // 8) * 8
    dma = pltpu.SemaphoreType.DMA
    vmem = pl.BlockSpec(memory_space=pltpu.VMEM)
    return pl.pallas_call(
        functools.partial(kernel, (E, N, rp, chunk, gather_w)),
        out_shape=(
            jax.ShapeDtypeStruct((rows, width), BF16),
            jax.ShapeDtypeStruct((1, 1, width, hidden), BF16),
            jax.ShapeDtypeStruct((1, shard, hidden), F32),
        ),
        in_specs=[vmem, vmem, vmem, vmem, pl.BlockSpec(memory_space=pl.ANY), vmem],
        out_specs=(vmem, vmem, vmem),
        scratch_shapes=[
            pltpu.VMEM((E, rows, width), BF16),
            pltpu.VMEM((E, rows, hidden), BF16),
            pltpu.VMEM((E, 8, rows), F32),
            pltpu.VMEM((width if gather_w else 16, hidden), BF16),
            pltpu.VMEM((E, rows, width), BF16),
            pltpu.VMEM((E, rows, hidden), BF16),
            pltpu.VMEM((width, hidden), BF16),
            pltpu.VMEM((width, hidden), F32),
            pltpu.VMEM((E, rows, width), BF16),
            pltpu.VMEM((E, rows, width), BF16),
            pltpu.VMEM((rp * N, 128), F32),
            pltpu.VMEM((N, rp, 128), F32),
            pltpu.VMEM((rp * N, 128), F32),
            pltpu.VMEM((N, rank, hidden), BF16),
            dma(()), dma((2 * E,)), dma((E,)), dma((E,)), dma((E,)), dma((E,)), dma((E,)),
            dma((N,)), dma((N,)), dma((N,)), dma((N,)), dma((N,)), dma((N,)), dma((N,)), dma((N,)),
            dma((E,)), dma((E,)),
        ],
        compiler_params=pltpu.CompilerParams(
            collective_id=0, has_side_effects=True, vmem_limit_bytes=67043328 - (1 << 20)),
    )(tokens, gh_sel, gate_sel, weight, error, q_seed[0].T)


def solution(mesh):
    placed = (
        P(("dp", "expert"), None),
        P(("dp", "expert"), None),
        P(("dp", "expert"), None),
        P(("dp", "expert"), None, None),
        P("expert", "dp", None),
        P("dp", "expert", None, None),
        P("expert", None, None),
    )
    return jax.shard_map(
        body,
        mesh=mesh,
        in_specs=placed,
        out_specs=(
            P(("dp", "expert"), None),
            P("dp", "expert", None, None),
            P("expert", "dp", None),
        ),
        check_vma=False,
    )
```

time: 213 us -> 106 us (0.50)
  Pallas kernels: 0 us -> 94.7 us
  waiting for transfers between devices: 76.5 us -> 0 us
  blocking collectives: 56.4 us -> 0 us
  matrix products: 22.3 us -> 0 us
  starting transfers between devices: 13.7 us -> 0 us
  between operations: 14.3 us -> 0.65 us
  other arithmetic: 14.6 us -> 1.02 us
  local copies, waits for them, and re-layouts: 14.4 us -> 9.14 us
    pallas_call x0 -> x1, Pallas kernels: none -> 94.7 us  [body(): pl.pallas_call(functools.partial(kernel, (E, N, rp, chunk, gather_w)), ou...]
    all_to_all x3 -> x0, waiting for transfers between devices: 48.8 us -> none  [the longest x1 41.6 us: body(): lax.all_to_all(sent_rows, 'expert', split_axis=0, concat_axis=0, tiled=True)]
    psum x2 -> x0, blocking collectives: 46.8 us -> none  [the longest x1 23.6 us: body(): lax.psum(jnp.dot(basis, merged, precision=highest).astype(jnp.bfloat16),...]
    unnamed x3 -> x0, waiting for transfers between devices: 27.7 us -> none
    dot_general x9 -> x0, matrix products: 22.1 us -> none  [the longest x1 4.22 us: body(): jnp.dot(basis, merged, precision=highest).astype(jnp.bfloat16)]
    all_to_all x3 -> x0, starting transfers between devices: 13.7 us -> none  [the longest x1 6.34 us: body(): lax.all_to_all(sent_grad, 'expert', split_axis=0, concat_axis=0, tiled=True)]
    all_gather x1 -> x0, blocking collectives: 9.58 us -> none  [body(): basis = lax.all_gather(part_basis, 'dp', axis=1, tiled=True)]
    another operation x7 -> x0, other arithmetic: 7.94 us -> none  [the longest x3 3.59 us: body(): lower_factor = jnp.linalg.cholesky(gram_matrix)]
  transfers between devices with their start and end apart: 5 -> 0, of which waited for: 3 -> 0; matrix products, arithmetic and copies ran while one was open for 14% -> 0% of each run, Pallas kernels for 0% -> 0%
where the time goes in v1:
time: 106 us
  Pallas kernels  94.7 us (89%)
  local copies, waits for them, and re-layouts  9.14 us (9%)
    pallas_call x1, Pallas kernels, body(): pl.pallas_call(functools.partial(kernel, (E, N, rp, chunk, gather_w)), ou...  94.7 us
    unnamed x5, local copies, waits for them, and re-layouts  5.49 us

profile of v1, /device:TPU:0, one launch (start us, length us, event | category | flops | bytes accessed | tf_op | source)
XLA Modules:
  0.0 105.5 jit_solution(5323566954352950310)
XLA Ops:
  0.6 0.8 slice_bitcast_fusion.3
  1.4 0.8 slice_bitcast_fusion.1
  2.2 0.6 broadcast_in_dim.86.gate_ref
  2.8 1.5 %fusion = (bf16[128,1,512]{2,1,0:T(2,128)(2,1)S(1)}, bf16[128,1,512]{2,1,0:T(2,128)(2,1)S(1)}) fusion(bf16[128,2,512]{2,1,0:T(2,128)(2,1)} %param.10), kind=kLoop, calls=%fused_computation.10 | loop fusion | bytes 524288 | tf_op jit(solution)/shard_map/slice | solution.py:272
  4.3 1.0 select_select_fusion.gh_ref
  5.3 94.7 %shard_map.94 = (bf16[128,1792]{1,0:T(8,128)(2,1)}, bf16[1,1,1792,512]{3,2,1,0:T(8,128)(2,1)}, f32[1,224,512]{2,1,0:T(8,128)}) custom-call(bf16[128,1792]{1,0:T(8,128)(2,1)} %tok_ref.1, bf16[4,128,512]{2,1,0:T(8,128)(2,1)} %select_select_fusion.gh_ref, f32[4,8,128]{2,1,0:T(8,128)} %broadcast_in_dim.86.gate_ref, bf16[224,512]{1,0:T(8,128)(2,1)} %bitcast.16, ...), custom_call_target="tpu_custom_call" | custom-call | tf_op jit(solution)/shard_map/pallas_call | solution.py:282
  100.0 1.8 %copy.19 = bf16[128,1792]{1,0:T(8,128)(2,1)} copy(bf16[128,1792]{1,0:T(8,128)(2,1)} %get-tuple-element.16) | data formatting | bytes 917504
  101.9 0.0 copy-start
  101.9 2.9 %copy.20 = bf16[1,1,1792,512]{3,2,1,0:T(8,128)(2,1)} copy(bf16[1,1,1792,512]{3,2,1,0:T(8,128)(2,1)} %get-tuple-element.17) | data formatting | bytes 3670016
  104.8 0.0 copy-done
  104.8 0.8 copy.21
  (3 shorter events, 0.1 us)
Async XLA Ops:
  101.9 2.9 %copy-start = (f32[1,224,512]{2,1,0:T(8,128)S(1)}, f32[1,224,512]{2,1,0:T(8,128)}, u32[]{:S(2)}) copy-start(f32[1,224,512]{2,1,0:T(8,128)} %get-tuple-element.18) | copy-start | bytes 1376260

commit v2 on v1

--- a/solution.py
+++ b/solution.py
@@ -39,7 +39,7 @@
 def kernel(dims, tok_ref, gh_ref, gate_ref, w_ref, err_hbm, qt_ref,
            gt_out, err_out, wg_out,
            tok_all, gh_all, gate_all, w_all, x_all, gp_all, err_v, merged, back, ret,
-           fbuf, rsbuf, agbuf, tbuf,
+           facc, fbuf, rsbuf, agbuf, tbuf,
            err_sem, tok_s, tok_r, gh_s, gh_r, gate_s, gate_r, w_s, w_r,
            f_s, f_r, a_s, a_r, t_s, t_r, b_s, b_r):
     E, N, rp, chunk, gather_w = dims
@@ -137,13 +137,38 @@
     tok_all[z] = tok_ref[...]
     gh_all[z] = gh_ref[z]
     gate_all[z] = gate_ref[z]
+    err_copy.wait()
+
+    def err_factor(c):
+        cols = pl.ds(pl.multiple_of(c * chunk, chunk), chunk)
+        facc[:, cols] = lax.dot_general(
+            qt_ref[...], err_v[cols, :].astype(F32), (((1,), (1,)), ((), ())), precision=HI,
+            preferred_element_type=F32)
+    loop(width // chunk, err_factor, 0)
     each("expert", E, gate_copy, "recv")
     forward(1, "relay")
     if gather_w:
         each("dp", N, w_copy, "recv")
 
-    def back_copy(p, slot, k):
-        return rdma(back.at[p], ret.at[slot], b_s.at[p], b_r.at[slot], "expert", p)
+    def back_copy(d):
+        dirn = jnp.where(d > z, 1, -1)
+        direct = (d - z) * dirn == E - 1
+        slot = jnp.where(direct, E + 1, jnp.where((d == z - 1), E, d))
+        return rdma(back.at[d], ret.at[slot], b_s.at[d], b_r.at[slot], "expert",
+                    jnp.where(direct, d, z + dirn))
+
+    def back_wait(slot):
+        rdma(back.at[0], ret.at[slot], b_s.at[0], b_r.at[slot], "expert",
+             other("expert", E, 1)).wait_recv()
+
+    def first_right(d):
+        return jnp.where(d == E - 1, 1, 0)
+
+    def first_left(d):
+        return jnp.where(d == 0, E - 2, E - 1)
+
+    def add_back(d, slot):
+        back[d] = (back[d].astype(F32) + ret[slot].astype(F32)).astype(BF16)
 
     def block(i, c):
         s = i // 2
@@ -166,19 +191,54 @@
             pre = jnp.dot(x, weights[...], preferred_element_type=F32)
             gp = (gh_all[j].astype(F32) * slopes(pre)).astype(BF16)
             gp_all[j] = gp
+            seen = lax.dot_general(gp.astype(F32), qt_ref[...], (((1,), (1,)), ((), ())),
+                                   precision=HI, preferred_element_type=F32)
+            facc[...] += lax.dot_general(seen, x.astype(F32), (((0,), (0,)), ((), ())),
+                                         precision=HI, preferred_element_type=F32)
             rows = lax.dot_general(gp, weights[...], (((1,), (1,)), ((), ())),
                                    preferred_element_type=F32)
             back[j] = (rows * g).astype(BF16)
 
-            @pl.when(s > 0)
+            @pl.when(((j > z) & (z <= first_right(j))) | ((j < z) & (z >= first_left(j))))
             def _():
-                back_copy(j, z, 0).start()
+                back_copy(j).start()
         return c
     lax.fori_loop(0, 2 * E, block, 0)
 
-    err_copy.wait()
     if fbuf.shape[0] > groups * rank:
         fbuf[...] = jnp.zeros_like(fbuf)
+    for c in range(groups):
+        fbuf[c * rank : (c + 1) * rank, :] = facc[:, c * 128 : (c + 1) * 128]
+
+    def f_copy(p, slot, k):
+        return rdma(fbuf.at[pl.ds(pl.multiple_of(p * rp, 8), rp)], rsbuf.at[slot],
+                    f_s.at[k], f_r.at[slot], "dp", p)
+
+    def a_copy(p, slot, k):
+        part = agbuf.at[pl.ds(pl.multiple_of(slot * rp, 8), rp)]
+        return rdma(part, part, a_s.at[k], a_r.at[slot], "dp", p)
+
+    def t_copy(p, slot, k):
+        return rdma(tbuf.at[slot], tbuf.at[slot], t_s.at[k], t_r.at[slot], "dp", p)
+
+    own = pl.ds(pl.multiple_of(me * rp, 8), rp)
+    each("dp", N, f_copy, "start")
+    rsbuf[me] = fbuf[own, :]
+    def relay_right(d):
+        @pl.when((d > z) & (z > first_right(d)))
+        def _():
+            back_wait(d)
+            add_back(d, d)
+            back_copy(d).start()
+    loop(E, relay_right, 0)
+
+    def relay_left(d):
+        @pl.when((d < z) & (z < first_left(d)))
+        def _():
+            back_wait(d)
+            add_back(d, d)
+            back_copy(d).start()
+    loop(E, relay_left, 0)
 
     def merge(c):
         cols = pl.ds(pl.multiple_of(c * chunk, chunk), chunk)
@@ -187,27 +247,8 @@
         m = lax.dot_general(x, gp, (((0,), (0,)), ((), ())), preferred_element_type=F32)
         m = m + err_v[cols, :].astype(F32)
         merged[cols, :] = m
-        f = lax.dot_general(qt_ref[...], m, (((1,), (1,)), ((), ())), precision=HI,
-                            preferred_element_type=F32)
-        for h in range(chunk // 128):
-            fbuf[pl.ds(pl.multiple_of((c * (chunk // 128) + h) * rank, rank), rank), :] = (
-                f[:, h * 128 : (h + 1) * 128])
     loop(width // chunk, merge, 0)
 
-    def f_copy(p, slot, k):
-        return rdma(fbuf.at[pl.ds(pl.multiple_of(p * rp, 8), rp)], rsbuf.at[slot],
-                    f_s.at[k], f_r.at[slot], "dp", p)
-
-    def a_copy(p, slot, k):
-        part = agbuf.at[pl.ds(pl.multiple_of(slot * rp, 8), rp)]
-        return rdma(part, part, a_s.at[k], a_r.at[slot], "dp", p)
-
-    def t_copy(p, slot, k):
-        return rdma(tbuf.at[slot], tbuf.at[slot], t_s.at[k], t_r.at[slot], "dp", p)
-
-    own = pl.ds(pl.multiple_of(me * rp, 8), rp)
-    each("dp", N, f_copy, "start")
-    rsbuf[me] = fbuf[own, :]
     each("dp", N, f_copy, "recv")
     agbuf[own, :] = jnp.sum(rsbuf[...], axis=0) * (1.0 / N)
     each("dp", N, a_copy, "start")
@@ -231,12 +272,21 @@
         merged[cols, :] = low
     wg_out[0] = merged[pl.ds(pl.multiple_of(me * shard, 8), shard), :]
 
-    each("expert", E, back_copy, "recv")
-    ret[z] = back[z]
-    total = ret[0].astype(F32)
-    for j in range(1, E):
-        total = total + ret[j].astype(F32)
-    gt_out[...] = total.astype(BF16)
+    @pl.when(z > first_right(z))
+    def _():
+        back_wait(z)
+        add_back(z, z)
+
+    @pl.when(z < first_left(z))
+    def _():
+        back_wait(E)
+        add_back(z, E)
+
+    @pl.when((z == 0) | (z == E - 1))
+    def _():
+        back_wait(E + 1)
+        add_back(z, E + 1)
+    gt_out[...] = back[z]
 
     forward_first = [(0, 1), (1, -1)]
     for d, dirn in forward_first:
@@ -250,7 +300,7 @@
     each("expert", E, gh_copy, "send")
     if gather_w:
         each("dp", N, w_copy, "send")
-    each("expert", E, back_copy, "send")
+    loop(E, lambda k: back_copy(other("expert", E, k)).wait_send())
     each("dp", N, f_copy, "send")
     each("dp", N, a_copy, "send")
     each("dp", N, t_copy, "send")
@@ -277,6 +327,7 @@
     total_rows = width // 128 * rank
     rp = -(-total_rows // N)
     rp = -(-rp // 8) * 8
+    room = (4 * E + 3) * rows * width * 2 + 3 * E * rows * hidden * 2 + 13 * width * hidden + (12 << 20)
     dma = pltpu.SemaphoreType.DMA
     vmem = pl.BlockSpec(memory_space=pltpu.VMEM)
     return pl.pallas_call(
@@ -298,17 +349,18 @@
             pltpu.VMEM((width, hidden), BF16),
             pltpu.VMEM((width, hidden), F32),
             pltpu.VMEM((E, rows, width), BF16),
-            pltpu.VMEM((E, rows, width), BF16),
+            pltpu.VMEM((E + 2, rows, width), BF16),
+            pltpu.VMEM((rank, width), F32),
             pltpu.VMEM((rp * N, 128), F32),
             pltpu.VMEM((N, rp, 128), F32),
             pltpu.VMEM((rp * N, 128), F32),
             pltpu.VMEM((N, rank, hidden), BF16),
             dma(()), dma((2 * E,)), dma((E,)), dma((E,)), dma((E,)), dma((E,)), dma((E,)),
             dma((N,)), dma((N,)), dma((N,)), dma((N,)), dma((N,)), dma((N,)), dma((N,)), dma((N,)),
-            dma((E,)), dma((E,)),
+            dma((E,)), dma((E + 2,)),
         ],
         compiler_params=pltpu.CompilerParams(
-            collective_id=0, has_side_effects=True, vmem_limit_bytes=67043328 - (1 << 20)),
+            collective_id=0, has_side_effects=True, vmem_limit_bytes=min(room, 67043328 - (1 << 20))),
     )(tokens, gh_sel, gate_sel, weight, error, q_seed[0].T)
 
 

time: 106 us -> 82.4 us (0.78)
  Pallas kernels: 94.7 us -> 75.2 us
  local copies, waits for them, and re-layouts: 9.14 us -> 5.93 us
    pallas_call x1, Pallas kernels: 94.7 us -> 75.2 us  [body(): pl.pallas_call(functools.partial(kernel, (E, N, rp, chunk, gather_w)), ou...]
    unnamed x5 -> x11, local copies, waits for them, and re-layouts: 5.49 us -> 2.78 us
where the time goes in v2:
time: 82.4 us; the launch traced here: 82.1 us
  Pallas kernels  75.2 us (91%)
  local copies, waits for them, and re-layouts  5.93 us (7%)
    pallas_call x1, Pallas kernels, body(): pl.pallas_call(functools.partial(kernel, (E, N, rp, chunk, gather_w)), ou...  75.2 us
    unnamed x11, local copies, waits for them, and re-layouts  2.78 us

profile of v2, /device:TPU:0, one launch (start us, length us, event | category | flops | bytes accessed | tf_op | source)
XLA Modules:
  0.0 82.1 jit_solution(14110445677107195854)
XLA Ops:
  0.6 0.0 copy-start.3
  0.6 0.0 copy-start
  0.7 0.0 copy-start.2
  0.7 0.0 copy-start.1
  0.7 0.8 %slice_bitcast_fusion.3 = (s32[128]{0:T(128)S(1)}, s32[128]{0:T(128)S(1)}) fusion(s32[128,2]{0,1:T(2,128)} %param.8), kind=kLoop, calls=%fused_computation.9 | loop fusion | bytes 2048 | tf_op jit(solution)/shard_map/eq | solution.py:317
  1.5 0.8 slice_bitcast_fusion.1
  2.3 1.5 %fusion = (bf16[128,1,512]{2,1,0:T(2,128)(2,1)S(1)}, bf16[128,1,512]{2,1,0:T(2,128)(2,1)S(1)}) fusion(bf16[128,2,512]{2,1,0:T(2,128)(2,1)} %param.10), kind=kLoop, calls=%fused_computation.10 | loop fusion | bytes 524288 | tf_op jit(solution)/shard_map/slice | solution.py:322
  3.8 0.2 select_select_fusion.gh_ref
  4.1 0.0 copy-done.3
  4.1 0.0 copy-done
  4.1 0.0 copy-done.2
  4.1 0.0 copy-done.1
  4.1 75.2 %shard_map.94 = (bf16[128,1792]{1,0:T(8,128)(2,1)S(1)}, bf16[1,1,1792,512]{3,2,1,0:T(8,128)(2,1)S(1)}, f32[1,224,512]{2,1,0:T(8,128)S(1)}) custom-call(bf16[128,1792]{1,0:T(8,128)(2,1)S(1)} %copy-done.1, bf16[4,128,512]{2,1,0:T(8,128)(2,1)S(1)} %select_select_fusion.gh_ref, f32[4,8,128]{2,1,0:T(8,128)S(1)} %broadcast_in_dim.86.gate_ref, ...), custom_call_target="tpu_custom_call" | custom-call | tf_op jit(solution)/shard_map/pallas_call | solution.py:333
  79.3 0.8 copy.19
  80.1 1.2 %copy.20 = bf16[1,1,1792,512]{3,2,1,0:T(8,128)(2,1)} copy(bf16[1,1,1792,512]{3,2,1,0:T(8,128)(2,1)S(1)} %get-tuple-element.17) | data formatting | bytes 3670016
  81.3 0.8 copy.21
  (4 shorter events, 0.1 us)
Async XLA Ops:
  0.6 3.4 %copy-start.3 = (f32[1,512,32]{1,2,0:T(8,128)S(1)}, f32[1,512,32]{1,2,0:T(8,128)}, u32[]{:S(2)}) copy-start(f32[1,512,32]{1,2,0:T(8,128)} %param.13) | copy-start | bytes 196612
  0.6 3.4 %copy-start = (bf16[1,1,1792,512]{3,2,1,0:T(8,128)(2,1)S(1)}, bf16[1,1,1792,512]{3,2,1,0:T(8,128)(2,1)}, u32[]{:S(2)}) copy-start(bf16[1,1,1792,512]{3,2,1,0:T(8,128)(2,1)} %err_hbm.1) | copy-start | bytes 5505028
  0.7 3.4 %copy-start.2 = (bf16[1,224,512]{2,1,0:T(8,128)(2,1)S(1)}, bf16[1,224,512]{2,1,0:T(8,128)(2,1)}, u32[]{:S(2)}) copy-start(bf16[1,224,512]{2,1,0:T(8,128)(2,1)} %param.11) | copy-start | bytes 688132
  0.7 3.4 %copy-start.1 = (bf16[128,1792]{1,0:T(8,128)(2,1)S(1)}, bf16[128,1792]{1,0:T(8,128)(2,1)}, u32[]{:S(2)}) copy-start(bf16[128,1792]{1,0:T(8,128)(2,1)} %tok_ref.1) | copy-start | bytes 1376260

commit v3 on v2

--- a/solution.py
+++ b/solution.py
@@ -25,15 +25,15 @@
     left = gram
     right = (rows == cols).astype(F32)
     row_id = lax.broadcasted_iota(jnp.int32, (rank, 1), 0)
-    for i in range(rank):
-        inv = 1.0 / jnp.sqrt(left[i : i + 1, i : i + 1])
-        row_l = left[i : i + 1, :] * inv
-        row_r = right[i : i + 1, :] * inv
-        col = jnp.where(row_id > i, left[:, i : i + 1] * inv, 0.0)
-        here = row_id == i
-        left = jnp.where(here, row_l, left - col * row_l)
-        right = jnp.where(here, row_r, right - col * row_r)
-    return right
+    for i in range(rank - 1):
+        scale = 1.0 / left[i : i + 1, i : i + 1]
+        col = jnp.where(row_id > i, left[:, i : i + 1], 0.0)
+        row_l = left[i : i + 1, :] * scale
+        row_r = right[i : i + 1, :] * scale
+        left = left - col * row_l
+        right = right - col * row_r
+    pivots = jnp.sum(jnp.where(rows == cols, left, 0.0), axis=1, keepdims=True)
+    return right * (1.0 / jnp.sqrt(pivots))
 
 
 def kernel(dims, tok_ref, gh_ref, gate_ref, w_ref, err_hbm, qt_ref,
@@ -257,16 +257,16 @@
     gram = lax.dot_general(factor, factor, (((1,), (1,)), ((), ())), precision=HI,
                            preferred_element_type=F32)
     basis = jnp.dot(inverse_factor(gram), factor, precision=HI, preferred_element_type=F32)
-    right = jnp.dot(basis, merged[...], precision=HI, preferred_element_type=F32)
+    right = jnp.dot(basis.astype(BF16), merged[...].astype(BF16), preferred_element_type=F32)
     tbuf[me] = right.astype(BF16)
     each("dp", N, t_copy, "start")
-    basis_t = jnp.transpose(basis)
+    basis_t = jnp.transpose(basis).astype(BF16)
     each("dp", N, t_copy, "recv")
-    q_factor = jnp.sum(tbuf[...].astype(F32), axis=0) * (1.0 / N)
+    q_factor = (jnp.sum(tbuf[...].astype(F32), axis=0) * (1.0 / N)).astype(BF16)
 
     for c in range(width // chunk):
         cols = pl.ds(c * chunk, chunk)
-        low = jnp.dot(basis_t[c * chunk : (c + 1) * chunk, :], q_factor, precision=HI,
+        low = jnp.dot(basis_t[c * chunk : (c + 1) * chunk, :], q_factor,
                       preferred_element_type=F32)
         err_out[0, 0, cols, :] = (merged[cols, :] - low).astype(BF16)
         merged[cols, :] = low

time: 82.4 us -> 80.7 us (0.979)
  Pallas kernels: 75.2 us -> 73.7 us
    pallas_call x1, Pallas kernels: 75.2 us -> 73.7 us  [body(): pl.pallas_call(functools.partial(kernel, (E, N, rp, chunk, gather_w)), ou...]
where the time goes in v3:
time: 80.7 us; the launch traced here: 80.5 us
  Pallas kernels  73.7 us (91%)
  local copies, waits for them, and re-layouts  5.93 us (7%)
    pallas_call x1, Pallas kernels, body(): pl.pallas_call(functools.partial(kernel, (E, N, rp, chunk, gather_w)), ou...  73.7 us
    unnamed x11, local copies, waits for them, and re-layouts  2.78 us

profile of v3, /device:TPU:0, one launch (start us, length us, event | category | flops | bytes accessed | tf_op | source)
XLA Modules:
  0.0 80.5 jit_solution(1865817217273529673)
XLA Ops:
  0.6 0.0 copy-start.3
  0.6 0.0 copy-start
  0.7 0.0 copy-start.2
  0.7 0.0 copy-start.1
  0.7 0.8 %slice_bitcast_fusion.3 = (s32[128]{0:T(128)S(1)}, s32[128]{0:T(128)S(1)}) fusion(s32[128,2]{0,1:T(2,128)} %param.8), kind=kLoop, calls=%fused_computation.9 | loop fusion | bytes 2048 | tf_op jit(solution)/shard_map/eq | solution.py:317
  1.5 0.8 slice_bitcast_fusion.1
  2.3 1.5 %fusion = (bf16[128,1,512]{2,1,0:T(2,128)(2,1)S(1)}, bf16[128,1,512]{2,1,0:T(2,128)(2,1)S(1)}) fusion(bf16[128,2,512]{2,1,0:T(2,128)(2,1)} %param.10), kind=kLoop, calls=%fused_computation.10 | loop fusion | bytes 524288 | tf_op jit(solution)/shard_map/slice | solution.py:322
  3.8 0.2 select_select_fusion.gh_ref
  4.1 0.0 copy-done.3
  4.1 0.0 copy-done
  4.1 0.0 copy-done.2
  4.1 0.0 copy-done.1
  4.1 73.7 %shard_map.94 = (bf16[128,1792]{1,0:T(8,128)(2,1)S(1)}, bf16[1,1,1792,512]{3,2,1,0:T(8,128)(2,1)S(1)}, f32[1,224,512]{2,1,0:T(8,128)S(1)}) custom-call(bf16[128,1792]{1,0:T(8,128)(2,1)S(1)} %copy-done.1, bf16[4,128,512]{2,1,0:T(8,128)(2,1)S(1)} %select_select_fusion.gh_ref, f32[4,8,128]{2,1,0:T(8,128)S(1)} %broadcast_in_dim.86.gate_ref, ...), custom_call_target="tpu_custom_call" | custom-call | tf_op jit(solution)/shard_map/pallas_call | solution.py:333
  77.8 0.8 copy.19
  78.5 1.2 %copy.20 = bf16[1,1,1792,512]{3,2,1,0:T(8,128)(2,1)} copy(bf16[1,1,1792,512]{3,2,1,0:T(8,128)(2,1)S(1)} %get-tuple-element.17) | data formatting | bytes 3670016
  79.8 0.8 copy.21
  (4 shorter events, 0.1 us)
Async XLA Ops:
  0.6 3.4 %copy-start.3 = (f32[1,512,32]{1,2,0:T(8,128)S(1)}, f32[1,512,32]{1,2,0:T(8,128)}, u32[]{:S(2)}) copy-start(f32[1,512,32]{1,2,0:T(8,128)} %param.13) | copy-start | bytes 196612
  0.6 3.4 %copy-start = (bf16[1,1,1792,512]{3,2,1,0:T(8,128)(2,1)S(1)}, bf16[1,1,1792,512]{3,2,1,0:T(8,128)(2,1)}, u32[]{:S(2)}) copy-start(bf16[1,1,1792,512]{3,2,1,0:T(8,128)(2,1)} %err_hbm.1) | copy-start | bytes 5505028
  0.7 3.4 %copy-start.2 = (bf16[1,224,512]{2,1,0:T(8,128)(2,1)S(1)}, bf16[1,224,512]{2,1,0:T(8,128)(2,1)}, u32[]{:S(2)}) copy-start(bf16[1,224,512]{2,1,0:T(8,128)(2,1)} %param.11) | copy-start | bytes 688132
  0.7 3.4 %copy-start.1 = (bf16[128,1792]{1,0:T(8,128)(2,1)S(1)}, bf16[128,1792]{1,0:T(8,128)(2,1)}, u32[]{:S(2)}) copy-start(bf16[128,1792]{1,0:T(8,128)(2,1)} %tok_ref.1) | copy-start | bytes 1376260
